TPU v7x, 32 devices: a whole 2x2x4 slice. The times are simulated.
32 devices in a mesh: group: 4 (over y, core), sub: 8 (over z, x).
Axes of the slice: x: 2, y: 2, z: 4, core: 2. Of those that a mesh axis runs over, the one named last changes fastest.
Arguments:
- shared_sizes: int32 [4, 8, 2], P('group', 'sub'), may hold values from 0 to 256, as said below
- stiffness: float32 [4, 8], P('group', 'sub'), may hold values from 0.1 to 10
- load_cases: float32 [4, 8, 1024, 384], P('group', 'sub'), may hold values from -6 to 6
- schur_blocks: bfloat16 [4, 8, 1024, 1024], P('group', 'sub')
- neumann_inverse: bfloat16 [4, 8, 1024, 1024], P('group', 'sub')
- coarse_basis: bfloat16 [4, 8, 32, 1024], P('group', 'sub'), may hold values from -0.1875 to 0.1875
- coarse_dofs: int32 [4, 8, 32], P('group', 'sub'), may hold values from 0 to 511
- coarse_inverse: float32 [512, 512], P('sub'), as said below
Outputs:
- solution: float32 [4, 8, 1024, 384], P('group', 'sub')
- residual: float32 [4, 8, 1024, 384], P('group', 'sub')
Inputs may be any that keep to these rules, and one draw needn't show every extreme that they name: shared_sizes[g, s, 0] equals shared_sizes[g, s - 1, 1]; the lower share of the first and the upper share of the last subdomain of a group are 0, the other shares lie in 128 to 256, and in every group some subdomain shares exactly 256 with its upper neighbour. `coarse_inverse`: symmetric.
All inputs are finite; a program needn't handle non-finite values.
Results may differ from a plain program's by a relative error of at most 0.0075.
Values sent between devices are 32-bit elements; how exact they have to be, the bound alone decides.
No kernel may reach another device: no remote copies, remote signals or barrier semaphores. Data moves between devices by JAX's collectives and lax.ppermute only.
A program may use at most 128 MiB of HBM per device.

v0:
```python
import jax
import jax.numpy as jnp
from jax import lax
from jax.sharding import PartitionSpec as P

MAXSH = 256
ITERS = 4
OMEGA = 0.6


def from_behind(block, axis, distance):
    devices = range(lax.axis_size(axis))
    route = [(i - distance, i) for i in devices if i - distance in devices]
    return lax.ppermute(block, axis, route)


def extended(x, sides, width):
    for axis, dim in sides:
        peers, length = (lax.axis_size(axis), x.shape[dim])
        up = [(i, (i + 1) % peers) for i in range(peers - 1)]
        down = [(j, i) for i, j in up]
        last = lax.slice_in_dim(x, length - width, length, axis=dim)
        leading = lax.slice_in_dim(x, 0, width, axis=dim)
        before = lax.ppermute(last, axis, up)
        after = lax.ppermute(leading, axis, down)
        x = jnp.concatenate([before, x, after], axis=dim)
    return x


def lift_piece(tail_rows, share_size):
    slab_width = tail_rows.shape[0]
    rolled = jnp.roll(tail_rows, share_size - slab_width, axis=0)
    inside = (jnp.arange(slab_width) < share_size)[:, None]
    return jnp.where(inside, rolled, jnp.zeros_like(rolled))


def place_piece(head_rows, share_size):
    slab_width = head_rows.shape[0]
    inside = (jnp.arange(slab_width) < share_size)[:, None]
    masked = jnp.where(inside, head_rows, jnp.zeros_like(head_rows))
    return jnp.roll(masked, slab_width - share_size, axis=0)


def assemble(vector, share_up):
    unknowns = vector.shape[0]
    tail_rows = vector[unknowns - MAXSH :]
    head_rows = vector[:MAXSH]
    lifted = lift_piece(tail_rows, share_up)
    from_lower = from_behind(lifted, "sub", 1)
    from_upper = from_behind(head_rows, "sub", -1)
    placed = place_piece(from_upper, share_up)
    return jnp.concatenate(
        [head_rows + from_lower, vector[MAXSH : unknowns - MAXSH], tail_rows + placed], axis=0
    )


def on_device(
    shared_sizes,
    stiffness,
    load_cases,
    schur_blocks,
    neumann_inverse,
    coarse_basis,
    coarse_dofs,
    coarse_inverse,
):
    share_low = shared_sizes[0, 0, 0]
    share_up = shared_sizes[0, 0, 1]
    beside_all = extended(stiffness, (("sub", 1),), 1)
    own_stiff = beside_all[0, 1]
    low_weight = own_stiff / (own_stiff + beside_all[0, 0])
    up_weight = own_stiff / (own_stiff + beside_all[0, 2])
    loads = load_cases[0, 0]
    schur = schur_blocks[0, 0]
    neumann = neumann_inverse[0, 0]
    basis = coarse_basis[0, 0]
    my_dofs = coarse_dofs[0, 0]
    unknowns, cases = loads.shape
    own_count = coarse_inverse.shape[0]
    row_index = jnp.arange(unknowns)
    weight = jnp.where(
        row_index < share_low,
        low_weight,
        jnp.where(row_index >= unknowns - share_up, up_weight, jnp.float32(1.0)),
    )[:, None]
    highest = lax.Precision.HIGHEST

    def operator_residual(solution):
        return loads - jnp.dot(
            schur, solution.astype(jnp.bfloat16), preferred_element_type=jnp.float32
        )

    solution = jnp.zeros((unknowns, cases), jnp.float32)
    for sweep in range(ITERS):
        local = operator_residual(solution)
        weighted = (weight * assemble(local, share_up)).astype(jnp.bfloat16)
        coarse_terms = jnp.dot(basis, weighted, preferred_element_type=jnp.float32)
        dof_values = my_dofs.astype(jnp.float32)
        all_terms = lax.all_gather(coarse_terms, "sub", axis=0, tiled=True)
        all_dofs = lax.all_gather(dof_values, "sub", axis=0, tiled=True)
        dof_index = all_dofs.astype(jnp.int32)
        first_row = lax.axis_index("sub") * own_count
        own_select = (dof_index[:, None] == first_row + jnp.arange(own_count)[None, :]).astype(
            jnp.float32
        )
        owned = lax.dot_general(own_select, all_terms, (((0,), (0,)), ((), ())), precision=highest)
        owned = lax.psum(owned, "group")
        columns = jnp.take(coarse_inverse, dof_index, axis=1)
        partial_vals = lax.dot_general(columns, owned, (((0,), (0,)), ((), ())), precision=highest)
        partial_vals = partial_vals.reshape(-1, coarse_terms.shape[0], cases)
        received = lax.all_to_all(partial_vals, "sub", split_axis=0, concat_axis=0, tiled=True)
        picked = jnp.sum(received, axis=0)
        picked = picked.astype(jnp.bfloat16)
        correction = jnp.dot(neumann, weighted, preferred_element_type=jnp.float32)
        correction = correction + lax.dot_general(
            basis, picked, (((0,), (0,)), ((), ())), preferred_element_type=jnp.float32
        )
        solution = solution + OMEGA * assemble(weight * correction, share_up)
    residual = assemble(operator_residual(solution), share_up)
    return (solution[None, None], residual[None, None])


def solution(mesh):
    return jax.shard_map(
        on_device,
        mesh=mesh,
        in_specs=(
            P("group", "sub", None),
            P("group", "sub"),
            P("group", "sub", None, None),
            P("group", "sub", None, None),
            P("group", "sub", None, None),
            P("group", "sub", None, None),
            P("group", "sub", None),
            P("sub", None),
        ),
        out_specs=(P("group", "sub", None, None), P("group", "sub", None, None)),
        check_vma=False,
    )
```

profile of v0, /device:TPU:16, one launch (start us, length us, event | category | flops | bytes accessed | tf_op | source)
XLA Modules:
  0.0 597.5 jit_solution(9661922671992732006)
XLA Ops:
  7.2 3.4 collective-permute-start.1
  20.8 4.2 collective-permute-start.3
  31.0 14.9 %all-reduce = f32[256]{0:T(256)S(1)} all-reduce(f32[256]{0:T(256)S(1)} %bitcast_dynamic-update-slice_fusion), channel_id=2, replica_groups=mesh['group'=4,'sub'=8] {'sub'}, use_global_device_ids=true, to_apply=%add | all-reduce | flops 256 | bytes 2048
  54.6 6.0 %collective-permute-done.2 = f32[256,384]{0,1:T(8,128)} collective-permute-done((f32[256,384]{0,1:T(8,128)}, f32[256,384]{0,1:T(8,128)}, u32[]{:S(2)}, u32[]{:S(2)}) %collective-permute-start.2) | collective-permute-done | bytes 393248 | tf_op jit(solution)/shard_map/ppermute | solution.py:14
  63.2 27.9 %all_gather.19 = f32[256,384]{1,0:T(8,128)S(1)} all-gather(f32[32,384]{1,0:T(8,128)S(1)} %convolution_bitcast_fusion.3), channel_id=1, replica_groups=mesh['group'=4,'sub'=8] {'sub'}, dimensions={0}, use_global_device_ids=true | all-gather | bytes 442368 | tf_op jit(solution)/shard_map/all_gather | solution.py:99
  93.1 34.8 %all-reduce.6.cloned.1.call-done = f32[64,384]{1,0:T(8,128)} async-done(((f32[64,384]{1,0:T(8,128)}), f32[64,384]{1,0:T(8,128)}) %all-reduce.6.cloned.1.call-update) | async-done | bytes 98320 | tf_op jit(solution)/shard_map/psum | solution.py:107
  129.4 15.0 %all_to_all.20 = f32[8,32,384]{2,1,0:T(8,128)} all-to-all(f32[8,32,384]{2,1,0:T(8,128)S(1)} %bitcast.145), channel_id=1, replica_groups=mesh['group'=4,'sub'=8] {'sub'}, dimensions={0} | all-to-all | bytes 786432 | tf_op jit(solution)/shard_map/all_to_all | solution.py:111
  152.3 8.6 %collective-permute-done.5 = f32[256,384]{0,1:T(8,128)S(1)} collective-permute-done((f32[256,384]{0,1:T(8,128)S(1)}, f32[256,384]{0,1:T(8,128)S(1)}, u32[]{:S(2)}, u32[]{:S(2)}) %collective-permute-start.5) | collective-permute-done | bytes 393248 | tf_op jit(solution)/shard_map/ppermute | solution.py:14
  165.2 7.9 %collective-permute-done.4 = f32[256,384]{0,1:T(8,128)S(1)} collective-permute-done((f32[256,384]{0,1:T(8,128)S(1)}, f32[256,384]{0,1:T(8,128)S(1)}, u32[]{:S(2)}, u32[]{:S(2)}) %collective-permute-start.4) | collective-permute-done | bytes 393248 | tf_op jit(solution)/shard_map/ppermute | solution.py:14
  176.5 8.2 %collective-permute-done.7 = f32[256,384]{0,1:T(8,128)S(1)} collective-permute-done((f32[256,384]{0,1:T(8,128)S(1)}, f32[256,384]{0,1:T(8,128)S(1)}, u32[]{:S(2)}, u32[]{:S(2)}) %collective-permute-start.7) | collective-permute-done | bytes 393248 | tf_op jit(solution)/shard_map/ppermute | solution.py:14
  187.6 8.1 %collective-permute-done.6 = f32[256,384]{0,1:T(8,128)S(1)} collective-permute-done((f32[256,384]{0,1:T(8,128)S(1)}, f32[256,384]{0,1:T(8,128)S(1)}, u32[]{:S(2)}, u32[]{:S(2)}) %collective-permute-start.6) | collective-permute-done | bytes 393248 | tf_op jit(solution)/shard_map/ppermute | solution.py:14
  196.3 25.4 %all_gather.20 = f32[256,384]{1,0:T(8,128)S(1)} all-gather(f32[32,384]{1,0:T(8,128)S(1)} %convolution_bitcast_fusion.2), channel_id=1, replica_groups=mesh['group'=4,'sub'=8] {'sub'}, dimensions={0}, use_global_device_ids=true | all-gather | bytes 442368 | tf_op jit(solution)/shard_map/all_gather | solution.py:99
  222.8 34.4 %all-reduce.8.cloned.1.call-done = f32[64,384]{1,0:T(8,128)} async-done(((f32[64,384]{1,0:T(8,128)}), f32[64,384]{1,0:T(8,128)}) %all-reduce.8.cloned.1.call-update) | async-done | bytes 98320 | tf_op jit(solution)/shard_map/psum | solution.py:107
  258.6 14.9 %all_to_all.21 = f32[8,32,384]{2,1,0:T(8,128)} all-to-all(f32[8,32,384]{2,1,0:T(8,128)S(1)} %bitcast.146), channel_id=1, replica_groups=mesh['group'=4,'sub'=8] {'sub'}, dimensions={0} | all-to-all | bytes 786432 | tf_op jit(solution)/shard_map/all_to_all | solution.py:111
  281.7 8.6 %collective-permute-done.9 = f32[256,384]{0,1:T(8,128)S(1)} collective-permute-done((f32[256,384]{0,1:T(8,128)S(1)}, f32[256,384]{0,1:T(8,128)S(1)}, u32[]{:S(2)}, u32[]{:S(2)}) %collective-permute-start.9) | collective-permute-done | bytes 393248 | tf_op jit(solution)/shard_map/ppermute | solution.py:14
  294.9 7.6 %collective-permute-done.8 = f32[256,384]{0,1:T(8,128)S(1)} collective-permute-done((f32[256,384]{0,1:T(8,128)S(1)}, f32[256,384]{0,1:T(8,128)S(1)}, u32[]{:S(2)}, u32[]{:S(2)}) %collective-permute-start.8) | collective-permute-done | bytes 393248 | tf_op jit(solution)/shard_map/ppermute | solution.py:14
  305.9 8.2 %collective-permute-done.11 = f32[256,384]{0,1:T(8,128)S(1)} collective-permute-done((f32[256,384]{0,1:T(8,128)S(1)}, f32[256,384]{0,1:T(8,128)S(1)}, u32[]{:S(2)}, u32[]{:S(2)}) %collective-permute-start.11) | collective-permute-done | bytes 393248 | tf_op jit(solution)/shard_map/ppermute | solution.py:14
  317.0 8.0 %collective-permute-done.10 = f32[256,384]{0,1:T(8,128)S(1)} collective-permute-done((f32[256,384]{0,1:T(8,128)S(1)}, f32[256,384]{0,1:T(8,128)S(1)}, u32[]{:S(2)}, u32[]{:S(2)}) %collective-permute-start.10) | collective-permute-done | bytes 393248 | tf_op jit(solution)/shard_map/ppermute | solution.py:14
  325.7 25.4 %all_gather.21 = f32[256,384]{1,0:T(8,128)S(1)} all-gather(f32[32,384]{1,0:T(8,128)S(1)} %convolution_bitcast_fusion.1), channel_id=1, replica_groups=mesh['group'=4,'sub'=8] {'sub'}, dimensions={0}, use_global_device_ids=true | all-gather | bytes 442368 | tf_op jit(solution)/shard_map/all_gather | solution.py:99
  352.2 34.4 %all-reduce.10.cloned.1.call-done = f32[64,384]{1,0:T(8,128)} async-done(((f32[64,384]{1,0:T(8,128)}), f32[64,384]{1,0:T(8,128)}) %all-reduce.10.cloned.1.call-update) | async-done | bytes 98320 | tf_op jit(solution)/shard_map/psum | solution.py:107
  388.0 14.9 %all_to_all.22 = f32[8,32,384]{2,1,0:T(8,128)} all-to-all(f32[8,32,384]{2,1,0:T(8,128)S(1)} %bitcast.147), channel_id=1, replica_groups=mesh['group'=4,'sub'=8] {'sub'}, dimensions={0} | all-to-all | bytes 786432 | tf_op jit(solution)/shard_map/all_to_all | solution.py:111
  411.1 8.6 %collective-permute-done.13 = f32[256,384]{0,1:T(8,128)S(1)} collective-permute-done((f32[256,384]{0,1:T(8,128)S(1)}, f32[256,384]{0,1:T(8,128)S(1)}, u32[]{:S(2)}, u32[]{:S(2)}) %collective-permute-start.13) | collective-permute-done | bytes 393248 | tf_op jit(solution)/shard_map/ppermute | solution.py:14
  424.0 7.9 %collective-permute-done.12 = f32[256,384]{0,1:T(8,128)S(1)} collective-permute-done((f32[256,384]{0,1:T(8,128)S(1)}, f32[256,384]{0,1:T(8,128)S(1)}, u32[]{:S(2)}, u32[]{:S(2)}) %collective-permute-start.12) | collective-permute-done | bytes 393248 | tf_op jit(solution)/shard_map/ppermute | solution.py:14
  435.4 8.2 %collective-permute-done.15 = f32[256,384]{0,1:T(8,128)S(1)} collective-permute-done((f32[256,384]{0,1:T(8,128)S(1)}, f32[256,384]{0,1:T(8,128)S(1)}, u32[]{:S(2)}, u32[]{:S(2)}) %collective-permute-start.15) | collective-permute-done | bytes 393248 | tf_op jit(solution)/shard_map/ppermute | solution.py:14
  446.5 8.1 %collective-permute-done.14 = f32[256,384]{0,1:T(8,128)S(1)} collective-permute-done((f32[256,384]{0,1:T(8,128)S(1)}, f32[256,384]{0,1:T(8,128)S(1)}, u32[]{:S(2)}, u32[]{:S(2)}) %collective-permute-start.14) | collective-permute-done | bytes 393248 | tf_op jit(solution)/shard_map/ppermute | solution.py:14
  455.2 25.4 %all_gather.22 = f32[256,384]{1,0:T(8,128)S(1)} all-gather(f32[32,384]{1,0:T(8,128)S(1)} %convolution_bitcast_fusion), channel_id=1, replica_groups=mesh['group'=4,'sub'=8] {'sub'}, dimensions={0}, use_global_device_ids=true | all-gather | bytes 442368 | tf_op jit(solution)/shard_map/all_gather | solution.py:99
  481.6 34.4 %all-reduce.12.cloned.1.call-done = f32[64,384]{1,0:T(8,128)} async-done(((f32[64,384]{1,0:T(8,128)}), f32[64,384]{1,0:T(8,128)}) %all-reduce.12.cloned.1.call-update) | async-done | bytes 98320 | tf_op jit(solution)/shard_map/psum | solution.py:107
  517.5 14.9 %all_to_all.23 = f32[8,32,384]{2,1,0:T(8,128)} all-to-all(f32[8,32,384]{2,1,0:T(8,128)S(1)} %bitcast.144), channel_id=1, replica_groups=mesh['group'=4,'sub'=8] {'sub'}, dimensions={0} | all-to-all | bytes 786432 | tf_op jit(solution)/shard_map/all_to_all | solution.py:111
  540.6 8.6 %collective-permute-done.17 = f32[256,384]{0,1:T(8,128)S(1)} collective-permute-done((f32[256,384]{0,1:T(8,128)S(1)}, f32[256,384]{0,1:T(8,128)S(1)}, u32[]{:S(2)}, u32[]{:S(2)}) %collective-permute-start.17) | collective-permute-done | bytes 393248 | tf_op jit(solution)/shard_map/ppermute | solution.py:14
  552.6 8.7 %collective-permute-done.16 = f32[256,384]{0,1:T(8,128)S(1)} collective-permute-done((f32[256,384]{0,1:T(8,128)S(1)}, f32[256,384]{0,1:T(8,128)S(1)}, u32[]{:S(2)}, u32[]{:S(2)}) %collective-permute-start.16) | collective-permute-done | bytes 393248 | tf_op jit(solution)/shard_map/ppermute | solution.py:14
  565.0 8.2 %collective-permute-done.19 = f32[256,384]{0,1:T(8,128)S(1)} collective-permute-done((f32[256,384]{0,1:T(8,128)S(1)}, f32[256,384]{0,1:T(8,128)S(1)}, u32[]{:S(2)}, u32[]{:S(2)}) %collective-permute-start.19) | collective-permute-done | bytes 393248 | tf_op jit(solution)/shard_map/ppermute | solution.py:14
  581.5 3.6 collective-permute-done.18
  (215 shorter events, 120.2 us)
Async XLA Ops:
  7.2 120.8 %all-reduce.6.cloned.1.call-start = ((), (), s32[]{:S(2)}) async-start(), calls=%async_computation.4 | async-start | bytes 196608 | tf_op jit(solution)/shard_map/psum | solution.py:107
  7.2 45.2 %collective-permute-start.1 = (f32[1,1]{1,0:T(1,128)}, f32[1,1]{1,0:T(1,128)}, u32[]{:S(2)}, u32[]{:S(2)}) collective-permute-start(f32[1,1]{1,0:T(1,128)} %param.13), channel_id=1, source_target_pairs={{1,0},{2,1},{3,2},{4,3},{5,4},{6,5},{7,6},{9,8},{10,9},{11,10},{12... | collective-permute-start | bytes 20 | tf_op jit(solution)/shard_map/ppermute | solution.py:25
  10.7 42.5 %collective-permute-start = (f32[1,1]{1,0:T(1,128)}, f32[1,1]{1,0:T(1,128)}, u32[]{:S(2)}, u32[]{:S(2)}) collective-permute-start(f32[1,1]{1,0:T(1,128)} %param.13), channel_id=1, source_target_pairs={{0,1},{1,2},{2,3},{3,4},{4,5},{5,6},{6,7},{8,9},{9,10},{10,11},{11... | collective-permute-start | bytes 20 | tf_op jit(solution)/shard_map/ppermute | solution.py:24
  20.8 25.8 %collective-permute-start.3 = (f32[256,384]{0,1:T(8,128)}, f32[256,384]{0,1:T(8,128)S(1)}, u32[]{:S(2)}, u32[]{:S(2)}) collective-permute-start(f32[256,384]{0,1:T(8,128)} %get-tuple-element.51), channel_id=1, source_target_pairs={{1,0},{2,1},{3,2},{4,3},{5,4},{6,5},{7,6},{9,8},{10,9},{11,10},{12... | collective-permute-start | bytes 1179656 | tf_op jit(solution)/shard_map/ppermute | solution.py:14
  49.6 13.3 %copy-start.40 = (bf16[1,1,32,1024]{3,2,1,0:T(8,128)(2,1)S(1)}, bf16[1,1,32,1024]{3,2,1,0:T(8,128)(2,1)}, u32[]{:S(2)}) copy-start(bf16[1,1,32,1024]{3,2,1,0:T(8,128)(2,1)} %param.17) | copy-start | bytes 196612
  49.6 11.0 %collective-permute-start.2 = (f32[256,384]{0,1:T(8,128)}, f32[256,384]{0,1:T(8,128)}, u32[]{:S(2)}, u32[]{:S(2)}) collective-permute-start(f32[256,384]{0,1:T(8,128)} %get-tuple-element.70), channel_id=1, source_target_pairs={{0,1},{1,2},{2,3},{3,4},{4,5},{5,6},{6,7},{8,9},{9,10},{10,11},{11... | collective-permute-start | bytes 1179656 | tf_op jit(solution)/shard_map/ppermute | solution.py:14
  62.8 29.4 %copy-start.47 = (f32[64,512]{1,0:T(8,128)S(1)}, f32[64,512]{1,0:T(8,128)}, u32[]{:S(2)}) copy-start(f32[64,512]{1,0:T(8,128)} %param.19) | copy-start | bytes 393220
  92.2 165.0 %all-reduce.8.cloned.1.call-start = ((), (), s32[]{:S(2)}) async-start(), calls=%async_computation.5 | async-start | bytes 196608 | tf_op jit(solution)/shard_map/psum | solution.py:107
  129.4 16.4 %copy-start.21 = (f32[256,384]{0,1:T(8,128)S(1)}, f32[256,384]{0,1:T(8,128)}, u32[]{:S(2)}) copy-start(f32[256,384]{0,1:T(8,128)} %copy-done.20) | copy-start | bytes 1179652
  149.1 11.8 %collective-permute-start.5 = (f32[256,384]{0,1:T(8,128)S(1)}, f32[256,384]{0,1:T(8,128)S(1)}, u32[]{:S(2)}, u32[]{:S(2)}) collective-permute-start(f32[256,384]{0,1:T(8,128)S(1)} %get-tuple-element.47), channel_id=1, source_target_pairs={{1,0},{2,1},{3,2},{4,3},{5,4},{6,5},{7,6},{9,8},{10,9},{11,10},{12... | collective-permute-start | bytes 1179656 | tf_op jit(solution)/shard_map/ppermute | solution.py:14
  161.2 11.9 %collective-permute-start.4 = (f32[256,384]{0,1:T(8,128)S(1)}, f32[256,384]{0,1:T(8,128)S(1)}, u32[]{:S(2)}, u32[]{:S(2)}) collective-permute-start(f32[256,384]{0,1:T(8,128)S(1)} %get-tuple-element.66), channel_id=1, source_target_pairs={{0,1},{1,2},{2,3},{3,4},{4,5},{5,6},{6,7},{8,9},{9,10},{10,11},{11... | collective-permute-start | bytes 1179656 | tf_op jit(solution)/shard_map/ppermute | solution.py:14
  174.6 10.1 %collective-permute-start.7 = (f32[256,384]{0,1:T(8,128)S(1)}, f32[256,384]{0,1:T(8,128)S(1)}, u32[]{:S(2)}, u32[]{:S(2)}) collective-permute-start(f32[256,384]{0,1:T(8,128)S(1)} %get-tuple-element.41), channel_id=1, source_target_pairs={{1,0},{2,1},{3,2},{4,3},{5,4},{6,5},{7,6},{9,8},{10,9},{11,10},{12... | collective-permute-start | bytes 1179656 | tf_op jit(solution)/shard_map/ppermute | solution.py:14
  185.0 10.7 %collective-permute-start.6 = (f32[256,384]{0,1:T(8,128)S(1)}, f32[256,384]{0,1:T(8,128)S(1)}, u32[]{:S(2)}, u32[]{:S(2)}) collective-permute-start(f32[256,384]{0,1:T(8,128)S(1)} %get-tuple-element.64), channel_id=1, source_target_pairs={{0,1},{1,2},{2,3},{3,4},{4,5},{5,6},{6,7},{8,9},{9,10},{10,11},{11... | collective-permute-start | bytes 1179656 | tf_op jit(solution)/shard_map/ppermute | solution.py:14
  195.9 25.8 %copy-start.26 = (f32[256,384]{0,1:T(8,128)}, f32[256,384]{0,1:T(8,128)S(1)}, u32[]{:S(2)}) copy-start(f32[256,384]{0,1:T(8,128)S(1)} %get-tuple-element.39) | copy-start | bytes 1179652
  222.7 163.8 %all-reduce.10.cloned.1.call-start = ((), (), s32[]{:S(2)}) async-start(), calls=%async_computation.6 | async-start | bytes 196608 | tf_op jit(solution)/shard_map/psum | solution.py:107
  278.5 11.8 %collective-permute-start.9 = (f32[256,384]{0,1:T(8,128)S(1)}, f32[256,384]{0,1:T(8,128)S(1)}, u32[]{:S(2)}, u32[]{:S(2)}) collective-permute-start(f32[256,384]{0,1:T(8,128)S(1)} %get-tuple-element.37), channel_id=1, source_target_pairs={{1,0},{2,1},{3,2},{4,3},{5,4},{6,5},{7,6},{9,8},{10,9},{11,10},{12... | collective-permute-start | bytes 1179656 | tf_op jit(solution)/shard_map/ppermute | solution.py:14
  290.6 11.9 %collective-permute-start.8 = (f32[256,384]{0,1:T(8,128)S(1)}, f32[256,384]{0,1:T(8,128)S(1)}, u32[]{:S(2)}, u32[]{:S(2)}) collective-permute-start(f32[256,384]{0,1:T(8,128)S(1)} %get-tuple-element.62), channel_id=1, source_target_pairs={{0,1},{1,2},{2,3},{3,4},{4,5},{5,6},{6,7},{8,9},{9,10},{10,11},{11... | collective-permute-start | bytes 1179656 | tf_op jit(solution)/shard_map/ppermute | solution.py:14
  303.9 10.1 %collective-permute-start.11 = (f32[256,384]{0,1:T(8,128)S(1)}, f32[256,384]{0,1:T(8,128)S(1)}, u32[]{:S(2)}, u32[]{:S(2)}) collective-permute-start(f32[256,384]{0,1:T(8,128)S(1)} %get-tuple-element.31), channel_id=1, source_target_pairs={{1,0},{2,1},{3,2},{4,3},{5,4},{6,5},{7,6},{9,8},{10,9},{11,10},{12... | collective-permute-start | bytes 1179656 | tf_op jit(solution)/shard_map/ppermute | solution.py:14
  314.3 10.7 %collective-permute-start.10 = (f32[256,384]{0,1:T(8,128)S(1)}, f32[256,384]{0,1:T(8,128)S(1)}, u32[]{:S(2)}, u32[]{:S(2)}) collective-permute-start(f32[256,384]{0,1:T(8,128)S(1)} %get-tuple-element.60), channel_id=1, source_target_pairs={{0,1},{1,2},{2,3},{3,4},{4,5},{5,6},{6,7},{8,9},{9,10},{10,11},{11... | collective-permute-start | bytes 1179656 | tf_op jit(solution)/shard_map/ppermute | solution.py:14
  325.3 25.8 %copy-start.28 = (f32[256,384]{0,1:T(8,128)}, f32[256,384]{0,1:T(8,128)S(1)}, u32[]{:S(2)}) copy-start(f32[256,384]{0,1:T(8,128)S(1)} %get-tuple-element.29) | copy-start | bytes 1179652
  352.1 163.9 %all-reduce.12.cloned.1.call-start = ((), (), s32[]{:S(2)}) async-start(), calls=%async_computation.7 | async-start | bytes 196608 | tf_op jit(solution)/shard_map/psum | solution.py:107
  407.9 11.9 %collective-permute-start.13 = (f32[256,384]{0,1:T(8,128)S(1)}, f32[256,384]{0,1:T(8,128)S(1)}, u32[]{:S(2)}, u32[]{:S(2)}) collective-permute-start(f32[256,384]{0,1:T(8,128)S(1)} %get-tuple-element.27), channel_id=1, source_target_pairs={{1,0},{2,1},{3,2},{4,3},{5,4},{6,5},{7,6},{9,8},{10,9},{11,10},{12... | collective-permute-start | bytes 1179656 | tf_op jit(solution)/shard_map/ppermute | solution.py:14
  420.0 11.9 %collective-permute-start.12 = (f32[256,384]{0,1:T(8,128)S(1)}, f32[256,384]{0,1:T(8,128)S(1)}, u32[]{:S(2)}, u32[]{:S(2)}) collective-permute-start(f32[256,384]{0,1:T(8,128)S(1)} %get-tuple-element.58), channel_id=1, source_target_pairs={{0,1},{1,2},{2,3},{3,4},{4,5},{5,6},{6,7},{8,9},{9,10},{10,11},{11... | collective-permute-start | bytes 1179656 | tf_op jit(solution)/shard_map/ppermute | solution.py:14
  433.4 10.1 %collective-permute-start.15 = (f32[256,384]{0,1:T(8,128)S(1)}, f32[256,384]{0,1:T(8,128)S(1)}, u32[]{:S(2)}, u32[]{:S(2)}) collective-permute-start(f32[256,384]{0,1:T(8,128)S(1)} %get-tuple-element.21), channel_id=1, source_target_pairs={{1,0},{2,1},{3,2},{4,3},{5,4},{6,5},{7,6},{9,8},{10,9},{11,10},{12... | collective-permute-start | bytes 1179656 | tf_op jit(solution)/shard_map/ppermute | solution.py:14
  443.9 10.7 %collective-permute-start.14 = (f32[256,384]{0,1:T(8,128)S(1)}, f32[256,384]{0,1:T(8,128)S(1)}, u32[]{:S(2)}, u32[]{:S(2)}) collective-permute-start(f32[256,384]{0,1:T(8,128)S(1)} %get-tuple-element.56), channel_id=1, source_target_pairs={{0,1},{1,2},{2,3},{3,4},{4,5},{5,6},{6,7},{8,9},{9,10},{10,11},{11... | collective-permute-start | bytes 1179656 | tf_op jit(solution)/shard_map/ppermute | solution.py:14
  454.8 25.8 %copy-start.24 = (f32[256,384]{0,1:T(8,128)}, f32[256,384]{0,1:T(8,128)S(1)}, u32[]{:S(2)}) copy-start(f32[256,384]{0,1:T(8,128)S(1)} %get-tuple-element.19) | copy-start | bytes 1179652
  537.3 11.8 %collective-permute-start.17 = (f32[256,384]{0,1:T(8,128)S(1)}, f32[256,384]{0,1:T(8,128)S(1)}, u32[]{:S(2)}, u32[]{:S(2)}) collective-permute-start(f32[256,384]{0,1:T(8,128)S(1)} %get-tuple-element.17), channel_id=1, source_target_pairs={{1,0},{2,1},{3,2},{4,3},{5,4},{6,5},{7,6},{9,8},{10,9},{11,10},{12... | collective-permute-start | bytes 1179656 | tf_op jit(solution)/shard_map/ppermute | solution.py:14
  549.2 12.5 %copy-start.45 = (f32[512,384]{0,1:T(8,128)S(1)}, f32[512,384]{0,1:T(8,128)}, u32[]{:S(2)}) copy-start(f32[512,384]{0,1:T(8,128)} %copy-done.44) | copy-start | bytes 2359300
  549.5 11.9 %collective-permute-start.16 = (f32[256,384]{0,1:T(8,128)S(1)}, f32[256,384]{0,1:T(8,128)S(1)}, u32[]{:S(2)}, u32[]{:S(2)}) collective-permute-start(f32[256,384]{0,1:T(8,128)S(1)} %get-tuple-element.54), channel_id=1, source_target_pairs={{0,1},{1,2},{2,3},{3,4},{4,5},{5,6},{6,7},{8,9},{9,10},{10,11},{11... | collective-permute-start | bytes 1179656 | tf_op jit(solution)/shard_map/ppermute | solution.py:14
  563.0 13.8 %copy-start.6 = (f32[1024,384]{0,1:T(8,128)}, f32[1024,384]{0,1:T(8,128)S(1)}, u32[]{:S(2)}) copy-start(f32[1024,384]{0,1:T(8,128)S(1)} %bitcast_subtract_fusion) | copy-start | bytes 4718596
  563.1 10.1 %collective-permute-start.19 = (f32[256,384]{0,1:T(8,128)S(1)}, f32[256,384]{0,1:T(8,128)S(1)}, u32[]{:S(2)}, u32[]{:S(2)}) collective-permute-start(f32[256,384]{0,1:T(8,128)S(1)} %get-tuple-element.11), channel_id=1, source_target_pairs={{1,0},{2,1},{3,2},{4,3},{5,4},{6,5},{7,6},{9,8},{10,9},{11,10},{12... | collective-permute-start | bytes 1179656 | tf_op jit(solution)/shard_map/ppermute | solution.py:14
  574.3 10.9 %collective-permute-start.18 = (f32[256,384]{0,1:T(8,128)}, f32[256,384]{0,1:T(8,128)}, u32[]{:S(2)}, u32[]{:S(2)}) collective-permute-start(f32[256,384]{0,1:T(8,128)} %get-tuple-element.52), channel_id=1, source_target_pairs={{0,1},{1,2},{2,3},{3,4},{4,5},{5,6},{6,7},{8,9},{9,10},{10,11},{11... | collective-permute-start | bytes 1179656 | tf_op jit(solution)/shard_map/ppermute | solution.py:14
  (44 other events, 245.8 us)
Sparse Core Ops, SparseCore 0:
  92.3 35.5 all-reduce.5
  222.9 34.2 all-reduce.7
  352.2 34.2 all-reduce.9
  481.7 34.2 all-reduce.11
where the time goes:
time: 599 us; the launch traced here: 598 us
  waiting for transfers between devices  271 us (45%)
  blocking collectives  179 us (30%)
  starting transfers between devices  55.8 us (9%)
  matrix products  30 us (5%)
  local copies, waits for them, and re-layouts  23.2 us (4%)
  between operations  19.8 us (3%)
  other arithmetic  18.8 us (3%)
    psum x4, waiting for transfers between devices, on_device(): owned = lax.psum(owned, 'group')  138 us
    ppermute x18, waiting for transfers between devices, from_behind(): return lax.ppermute(block, axis, route)  133 us
    all_gather x4, blocking collectives, on_device(): all_terms = lax.all_gather(coarse_terms, 'sub', axis=0, tiled=True)  104 us
    all_to_all x4, blocking collectives, on_device(): lax.all_to_all(partial_vals, 'sub', split_axis=0, concat_axis=0, tiled=True)  59.6 us
    ppermute x18, starting transfers between devices, from_behind(): return lax.ppermute(block, axis, route)  49.6 us
    unnamed x108, local copies, waits for them, and re-layouts  15.7 us
    unnamed x1, blocking collectives  14.9 us
  transfers between devices with their start and end apart: 24, of which 21 were waited for; matrix products, arithmetic and copies ran while one was open for 4% of the time, Pallas kernels for 0%

commit v1 on v0

--- a/solution.py
+++ b/solution.py
@@ -104,7 +104,9 @@
             jnp.float32
         )
         owned = lax.dot_general(own_select, all_terms, (((0,), (0,)), ((), ())), precision=highest)
-        owned = lax.psum(owned, "group")
+        owned = owned
+        for hop in (1, 2):
+            owned = owned + lax.ppermute(owned, "group", [(dev, dev ^ hop) for dev in range(4)])
         columns = jnp.take(coarse_inverse, dof_index, axis=1)
         partial_vals = lax.dot_general(columns, owned, (((0,), (0,)), ((), ())), precision=highest)
         partial_vals = partial_vals.reshape(-1, coarse_terms.shape[0], cases)

time: 599 us -> 482 us (0.80)
  waiting for transfers between devices: 271 us -> 150 us
  blocking collectives: 179 us -> 194 us
  between operations: 19.8 us -> 6.26 us
  starting transfers between devices: 55.8 us -> 64 us
    psum x4 -> x0, waiting for transfers between devices: 138 us -> none  [on_device(): owned = lax.psum(owned, 'group')]
    ppermute x0 -> x8, waiting for transfers between devices: none -> 17.3 us  [on_device(): lax.ppermute(owned, 'group', [(dev, dev ^ hop) for dev in range(4)])]
    all_to_all x4, blocking collectives: 59.6 us -> 72.6 us  [on_device(): lax.all_to_all(partial_vals, 'sub', split_axis=0, concat_axis=0, tiled=True)]
    ppermute x0 -> x8, starting transfers between devices: none -> 7.19 us  [on_device(): lax.ppermute(owned, 'group', [(dev, dev ^ hop) for dev in range(4)])]
  transfers between devices with their start and end apart: 24 -> 28, of which waited for: 21 -> 25; matrix products, arithmetic and copies ran while one was open for 4% -> 4% of each run, Pallas kernels for 0% -> 0%
where the time goes in v1:
time: 482 us; the launch traced here: 480 us
  blocking collectives  194 us (40%)
  waiting for transfers between devices  150 us (31%)
  starting transfers between devices  64 us (13%)
  matrix products  24.7 us (5%)
  local copies, waits for them, and re-layouts  22.4 us (5%)
  other arithmetic  19.6 us (4%)
  between operations  6.26 us (1%)
    ppermute x18, waiting for transfers between devices, from_behind(): return lax.ppermute(block, axis, route)  132 us
    all_gather x4, blocking collectives, on_device(): all_terms = lax.all_gather(coarse_terms, 'sub', axis=0, tiled=True)  106 us
    all_to_all x4, blocking collectives, on_device(): lax.all_to_all(partial_vals, 'sub', split_axis=0, concat_axis=0, tiled=True)  72.6 us
    ppermute x18, starting transfers between devices, from_behind(): return lax.ppermute(block, axis, route)  50.9 us
    ppermute x8, waiting for transfers between devices, on_device(): lax.ppermute(owned, 'group', [(dev, dev ^ hop) for dev in range(4)])  17.3 us
    unnamed x108, local copies, waits for them, and re-layouts  15 us
    unnamed x1, blocking collectives  14.8 us
    dot_general x4, matrix products, on_device(): correction = jnp.dot(neumann, weighted, preferred_element_type=jnp.float32)  10.6 us
  transfers between devices with their start and end apart: 28, of which 25 were waited for; matrix products, arithmetic and copies ran while one was open for 4% of the time, Pallas kernels for 0%

profile of v1, /device:TPU:16, one launch (start us, length us, event | category | flops | bytes accessed | tf_op | source)
XLA Modules:
  0.0 480.1 jit_solution(12757094747064048575)
XLA Ops:
  0.6 3.4 collective-permute-start.1
  14.2 4.2 collective-permute-start.3
  24.0 14.8 %all-reduce = f32[256]{0:T(256)S(1)} all-reduce(f32[256]{0:T(256)S(1)} %bitcast_dynamic-update-slice_fusion), channel_id=2, replica_groups=mesh['group'=4,'sub'=8] {'sub'}, use_global_device_ids=true, to_apply=%add | all-reduce | flops 256 | bytes 2048
  47.2 6.2 %collective-permute-done.2 = f32[256,384]{0,1:T(8,128)} collective-permute-done((f32[256,384]{0,1:T(8,128)}, f32[256,384]{0,1:T(8,128)}, u32[]{:S(2)}, u32[]{:S(2)}) %collective-permute-start.2) | collective-permute-done | bytes 393248 | tf_op jit(solution)/shard_map/ppermute | solution.py:14
  55.3 28.0 %all_gather.19 = f32[256,384]{1,0:T(8,128)S(1)} all-gather(f32[32,384]{1,0:T(8,128)S(1)} %convolution_bitcast_fusion.3), channel_id=1, replica_groups=mesh['group'=4,'sub'=8] {'sub'}, dimensions={0}, use_global_device_ids=true | all-gather | bytes 442368 | tf_op jit(solution)/shard_map/all_gather | solution.py:99
  92.6 18.8 %all_to_all.20 = f32[8,32,384]{2,1,0:T(8,128)} all-to-all(f32[8,32,384]{2,1,0:T(8,128)S(1)} %bitcast.141), channel_id=1, replica_groups=mesh['group'=4,'sub'=8] {'sub'}, dimensions={0} | all-to-all | bytes 786432 | tf_op jit(solution)/shard_map/all_to_all | solution.py:113
  116.1 3.2 collective-permute-start.7
  119.3 8.6 %collective-permute-done.7 = f32[256,384]{0,1:T(8,128)S(1)} collective-permute-done((f32[256,384]{0,1:T(8,128)S(1)}, f32[256,384]{0,1:T(8,128)S(1)}, u32[]{:S(2)}, u32[]{:S(2)}) %collective-permute-start.7) | collective-permute-done | bytes 393248 | tf_op jit(solution)/shard_map/ppermute | solution.py:14
  132.3 7.9 %collective-permute-done.6 = f32[256,384]{0,1:T(8,128)S(1)} collective-permute-done((f32[256,384]{0,1:T(8,128)S(1)}, f32[256,384]{0,1:T(8,128)S(1)}, u32[]{:S(2)}, u32[]{:S(2)}) %collective-permute-start.6) | collective-permute-done | bytes 393248 | tf_op jit(solution)/shard_map/ppermute | solution.py:14
  143.5 8.2 %collective-permute-done.9 = f32[256,384]{0,1:T(8,128)S(1)} collective-permute-done((f32[256,384]{0,1:T(8,128)S(1)}, f32[256,384]{0,1:T(8,128)S(1)}, u32[]{:S(2)}, u32[]{:S(2)}) %collective-permute-start.9) | collective-permute-done | bytes 393248 | tf_op jit(solution)/shard_map/ppermute | solution.py:14
  154.7 7.9 %collective-permute-done.8 = f32[256,384]{0,1:T(8,128)S(1)} collective-permute-done((f32[256,384]{0,1:T(8,128)S(1)}, f32[256,384]{0,1:T(8,128)S(1)}, u32[]{:S(2)}, u32[]{:S(2)}) %collective-permute-start.8) | collective-permute-done | bytes 393248 | tf_op jit(solution)/shard_map/ppermute | solution.py:14
  163.3 26.1 %all_gather.20 = f32[256,384]{1,0:T(8,128)S(1)} all-gather(f32[32,384]{1,0:T(8,128)S(1)} %convolution_bitcast_fusion.2), channel_id=1, replica_groups=mesh['group'=4,'sub'=8] {'sub'}, dimensions={0}, use_global_device_ids=true | all-gather | bytes 442368 | tf_op jit(solution)/shard_map/all_gather | solution.py:99
  196.6 17.9 %all_to_all.21 = f32[8,32,384]{2,1,0:T(8,128)} all-to-all(f32[8,32,384]{2,1,0:T(8,128)S(1)} %bitcast.142), channel_id=1, replica_groups=mesh['group'=4,'sub'=8] {'sub'}, dimensions={0} | all-to-all | bytes 786432 | tf_op jit(solution)/shard_map/all_to_all | solution.py:113
  219.5 3.3 collective-permute-start.13
  222.7 8.6 %collective-permute-done.13 = f32[256,384]{0,1:T(8,128)S(1)} collective-permute-done((f32[256,384]{0,1:T(8,128)S(1)}, f32[256,384]{0,1:T(8,128)S(1)}, u32[]{:S(2)}, u32[]{:S(2)}) %collective-permute-start.13) | collective-permute-done | bytes 393248 | tf_op jit(solution)/shard_map/ppermute | solution.py:14
  235.9 7.6 %collective-permute-done.12 = f32[256,384]{0,1:T(8,128)S(1)} collective-permute-done((f32[256,384]{0,1:T(8,128)S(1)}, f32[256,384]{0,1:T(8,128)S(1)}, u32[]{:S(2)}, u32[]{:S(2)}) %collective-permute-start.12) | collective-permute-done | bytes 393248 | tf_op jit(solution)/shard_map/ppermute | solution.py:14
  246.9 8.2 %collective-permute-done.15 = f32[256,384]{0,1:T(8,128)S(1)} collective-permute-done((f32[256,384]{0,1:T(8,128)S(1)}, f32[256,384]{0,1:T(8,128)S(1)}, u32[]{:S(2)}, u32[]{:S(2)}) %collective-permute-start.15) | collective-permute-done | bytes 393248 | tf_op jit(solution)/shard_map/ppermute | solution.py:14
  258.2 7.9 %collective-permute-done.14 = f32[256,384]{0,1:T(8,128)S(1)} collective-permute-done((f32[256,384]{0,1:T(8,128)S(1)}, f32[256,384]{0,1:T(8,128)S(1)}, u32[]{:S(2)}, u32[]{:S(2)}) %collective-permute-start.14) | collective-permute-done | bytes 393248 | tf_op jit(solution)/shard_map/ppermute | solution.py:14
  266.7 25.9 %all_gather.21 = f32[256,384]{1,0:T(8,128)S(1)} all-gather(f32[32,384]{1,0:T(8,128)S(1)} %convolution_bitcast_fusion.1), channel_id=1, replica_groups=mesh['group'=4,'sub'=8] {'sub'}, dimensions={0}, use_global_device_ids=true | all-gather | bytes 442368 | tf_op jit(solution)/shard_map/all_gather | solution.py:99
  299.9 18.0 %all_to_all.22 = f32[8,32,384]{2,1,0:T(8,128)} all-to-all(f32[8,32,384]{2,1,0:T(8,128)S(1)} %bitcast.143), channel_id=1, replica_groups=mesh['group'=4,'sub'=8] {'sub'}, dimensions={0} | all-to-all | bytes 786432 | tf_op jit(solution)/shard_map/all_to_all | solution.py:113
  322.9 3.2 collective-permute-start.19
  326.1 8.6 %collective-permute-done.19 = f32[256,384]{0,1:T(8,128)S(1)} collective-permute-done((f32[256,384]{0,1:T(8,128)S(1)}, f32[256,384]{0,1:T(8,128)S(1)}, u32[]{:S(2)}, u32[]{:S(2)}) %collective-permute-start.19) | collective-permute-done | bytes 393248 | tf_op jit(solution)/shard_map/ppermute | solution.py:14
  339.1 7.8 %collective-permute-done.18 = f32[256,384]{0,1:T(8,128)S(1)} collective-permute-done((f32[256,384]{0,1:T(8,128)S(1)}, f32[256,384]{0,1:T(8,128)S(1)}, u32[]{:S(2)}, u32[]{:S(2)}) %collective-permute-start.18) | collective-permute-done | bytes 393248 | tf_op jit(solution)/shard_map/ppermute | solution.py:14
  350.4 8.2 %collective-permute-done.21 = f32[256,384]{0,1:T(8,128)S(1)} collective-permute-done((f32[256,384]{0,1:T(8,128)S(1)}, f32[256,384]{0,1:T(8,128)S(1)}, u32[]{:S(2)}, u32[]{:S(2)}) %collective-permute-start.21) | collective-permute-done | bytes 393248 | tf_op jit(solution)/shard_map/ppermute | solution.py:14
  361.6 7.9 %collective-permute-done.20 = f32[256,384]{0,1:T(8,128)S(1)} collective-permute-done((f32[256,384]{0,1:T(8,128)S(1)}, f32[256,384]{0,1:T(8,128)S(1)}, u32[]{:S(2)}, u32[]{:S(2)}) %collective-permute-start.20) | collective-permute-done | bytes 393248 | tf_op jit(solution)/shard_map/ppermute | solution.py:14
  370.2 26.1 %all_gather.22 = f32[256,384]{1,0:T(8,128)S(1)} all-gather(f32[32,384]{1,0:T(8,128)S(1)} %convolution_bitcast_fusion), channel_id=1, replica_groups=mesh['group'=4,'sub'=8] {'sub'}, dimensions={0}, use_global_device_ids=true | all-gather | bytes 442368 | tf_op jit(solution)/shard_map/all_gather | solution.py:99
  403.5 17.9 %all_to_all.23 = f32[8,32,384]{2,1,0:T(8,128)} all-to-all(f32[8,32,384]{2,1,0:T(8,128)S(1)} %bitcast.140), channel_id=1, replica_groups=mesh['group'=4,'sub'=8] {'sub'}, dimensions={0} | all-to-all | bytes 786432 | tf_op jit(solution)/shard_map/all_to_all | solution.py:113
  426.4 3.3 collective-permute-start.25
  429.7 8.6 %collective-permute-done.25 = f32[256,384]{0,1:T(8,128)S(1)} collective-permute-done((f32[256,384]{0,1:T(8,128)S(1)}, f32[256,384]{0,1:T(8,128)S(1)}, u32[]{:S(2)}, u32[]{:S(2)}) %collective-permute-start.25) | collective-permute-done | bytes 393248 | tf_op jit(solution)/shard_map/ppermute | solution.py:14
  442.0 8.5 %collective-permute-done.24 = f32[256,384]{0,1:T(8,128)S(1)} collective-permute-done((f32[256,384]{0,1:T(8,128)S(1)}, f32[256,384]{0,1:T(8,128)S(1)}, u32[]{:S(2)}, u32[]{:S(2)}) %collective-permute-start.24) | collective-permute-done | bytes 393248 | tf_op jit(solution)/shard_map/ppermute | solution.py:14
  454.1 8.2 %collective-permute-done.27 = f32[256,384]{0,1:T(8,128)S(1)} collective-permute-done((f32[256,384]{0,1:T(8,128)S(1)}, f32[256,384]{0,1:T(8,128)S(1)}, u32[]{:S(2)}, u32[]{:S(2)}) %collective-permute-start.27) | collective-permute-done | bytes 393248 | tf_op jit(solution)/shard_map/ppermute | solution.py:14
  470.8 3.5 collective-permute-done.26
  (223 shorter events, 127.4 us)
Async XLA Ops:
  0.6 44.6 %collective-permute-start.1 = (f32[1,1]{1,0:T(1,128)}, f32[1,1]{1,0:T(1,128)}, u32[]{:S(2)}, u32[]{:S(2)}) collective-permute-start(f32[1,1]{1,0:T(1,128)} %param.13), channel_id=1, source_target_pairs={{1,0},{2,1},{3,2},{4,3},{5,4},{6,5},{7,6},{9,8},{10,9},{11,10},{12... | collective-permute-start | bytes 20 | tf_op jit(solution)/shard_map/ppermute | solution.py:25
  4.1 41.8 %collective-permute-start = (f32[1,1]{1,0:T(1,128)}, f32[1,1]{1,0:T(1,128)}, u32[]{:S(2)}, u32[]{:S(2)}) collective-permute-start(f32[1,1]{1,0:T(1,128)} %param.13), channel_id=1, source_target_pairs={{0,1},{1,2},{2,3},{3,4},{4,5},{5,6},{6,7},{8,9},{9,10},{10,11},{11... | collective-permute-start | bytes 20 | tf_op jit(solution)/shard_map/ppermute | solution.py:24
  14.2 25.2 %collective-permute-start.3 = (f32[256,384]{0,1:T(8,128)}, f32[256,384]{0,1:T(8,128)S(1)}, u32[]{:S(2)}, u32[]{:S(2)}) collective-permute-start(f32[256,384]{0,1:T(8,128)} %get-tuple-element.51), channel_id=1, source_target_pairs={{1,0},{2,1},{3,2},{4,3},{5,4},{6,5},{7,6},{9,8},{10,9},{11,10},{12... | collective-permute-start | bytes 1179656 | tf_op jit(solution)/shard_map/ppermute | solution.py:14
  42.4 11.0 %collective-permute-start.2 = (f32[256,384]{0,1:T(8,128)}, f32[256,384]{0,1:T(8,128)}, u32[]{:S(2)}, u32[]{:S(2)}) collective-permute-start(f32[256,384]{0,1:T(8,128)} %get-tuple-element.70), channel_id=1, source_target_pairs={{0,1},{1,2},{2,3},{3,4},{4,5},{5,6},{6,7},{8,9},{9,10},{10,11},{11... | collective-permute-start | bytes 1179656 | tf_op jit(solution)/shard_map/ppermute | solution.py:14
  54.9 28.8 %copy-start.20 = (f32[256,384]{0,1:T(8,128)}, f32[256,384]{0,1:T(8,128)S(1)}, u32[]{:S(2)}) copy-start(f32[256,384]{0,1:T(8,128)S(1)} %get-tuple-element.48) | copy-start | bytes 1179652
  54.9 28.8 %copy-start.22 = (f32[256,384]{0,1:T(8,128)}, f32[256,384]{0,1:T(8,128)S(1)}, u32[]{:S(2)}) copy-start(f32[256,384]{0,1:T(8,128)S(1)} %get-tuple-element.49) | copy-start | bytes 1179652
  55.0 28.9 %copy-start.47 = (f32[64,512]{1,0:T(8,128)S(1)}, f32[64,512]{1,0:T(8,128)}, u32[]{:S(2)}) copy-start(f32[64,512]{1,0:T(8,128)} %param.19) | copy-start | bytes 393220
  83.7 1.5 collective-permute-start.4
  86.1 5.0 %collective-permute-start.5 = (f32[64,384]{1,0:T(8,128)S(1)}, f32[64,384]{1,0:T(8,128)}, u32[]{:S(2)}, u32[]{:S(2)}) collective-permute-start(f32[64,384]{1,0:T(8,128)S(1)} %add.174), channel_id=1, source_target_pairs={{0,16},{8,24},{16,0},{24,8},{1,17},{9,25},{17,1},{25,9},{2,18},{10... | collective-permute-start | bytes 294920 | tf_op jit(solution)/shard_map/ppermute | solution.py:109
  116.1 11.9 %collective-permute-start.7 = (f32[256,384]{0,1:T(8,128)S(1)}, f32[256,384]{0,1:T(8,128)S(1)}, u32[]{:S(2)}, u32[]{:S(2)}) collective-permute-start(f32[256,384]{0,1:T(8,128)S(1)} %get-tuple-element.47), channel_id=1, source_target_pairs={{1,0},{2,1},{3,2},{4,3},{5,4},{6,5},{7,6},{9,8},{10,9},{11,10},{12... | collective-permute-start | bytes 1179656 | tf_op jit(solution)/shard_map/ppermute | solution.py:14
  128.2 11.9 %collective-permute-start.6 = (f32[256,384]{0,1:T(8,128)S(1)}, f32[256,384]{0,1:T(8,128)S(1)}, u32[]{:S(2)}, u32[]{:S(2)}) collective-permute-start(f32[256,384]{0,1:T(8,128)S(1)} %get-tuple-element.66), channel_id=1, source_target_pairs={{0,1},{1,2},{2,3},{3,4},{4,5},{5,6},{6,7},{8,9},{9,10},{10,11},{11... | collective-permute-start | bytes 1179656 | tf_op jit(solution)/shard_map/ppermute | solution.py:14
  141.5 10.1 %collective-permute-start.9 = (f32[256,384]{0,1:T(8,128)S(1)}, f32[256,384]{0,1:T(8,128)S(1)}, u32[]{:S(2)}, u32[]{:S(2)}) collective-permute-start(f32[256,384]{0,1:T(8,128)S(1)} %get-tuple-element.41), channel_id=1, source_target_pairs={{1,0},{2,1},{3,2},{4,3},{5,4},{6,5},{7,6},{9,8},{10,9},{11,10},{12... | collective-permute-start | bytes 1179656 | tf_op jit(solution)/shard_map/ppermute | solution.py:14
  152.0 10.7 %collective-permute-start.8 = (f32[256,384]{0,1:T(8,128)S(1)}, f32[256,384]{0,1:T(8,128)S(1)}, u32[]{:S(2)}, u32[]{:S(2)}) collective-permute-start(f32[256,384]{0,1:T(8,128)S(1)} %get-tuple-element.64), channel_id=1, source_target_pairs={{0,1},{1,2},{2,3},{3,4},{4,5},{5,6},{6,7},{8,9},{9,10},{10,11},{11... | collective-permute-start | bytes 1179656 | tf_op jit(solution)/shard_map/ppermute | solution.py:14
  189.8 1.4 collective-permute-start.10
  191.1 4.9 %collective-permute-start.11 = (f32[64,384]{1,0:T(8,128)S(1)}, f32[64,384]{1,0:T(8,128)S(1)}, u32[]{:S(2)}, u32[]{:S(2)}) collective-permute-start(f32[64,384]{1,0:T(8,128)S(1)} %add.181), channel_id=1, source_target_pairs={{0,16},{8,24},{16,0},{24,8},{1,17},{9,25},{17,1},{25,9},{2,18},{10... | collective-permute-start | bytes 294920 | tf_op jit(solution)/shard_map/ppermute | solution.py:109
  219.5 11.9 %collective-permute-start.13 = (f32[256,384]{0,1:T(8,128)S(1)}, f32[256,384]{0,1:T(8,128)S(1)}, u32[]{:S(2)}, u32[]{:S(2)}) collective-permute-start(f32[256,384]{0,1:T(8,128)S(1)} %get-tuple-element.37), channel_id=1, source_target_pairs={{1,0},{2,1},{3,2},{4,3},{5,4},{6,5},{7,6},{9,8},{10,9},{11,10},{12... | collective-permute-start | bytes 1179656 | tf_op jit(solution)/shard_map/ppermute | solution.py:14
  231.6 11.9 %collective-permute-start.12 = (f32[256,384]{0,1:T(8,128)S(1)}, f32[256,384]{0,1:T(8,128)S(1)}, u32[]{:S(2)}, u32[]{:S(2)}) collective-permute-start(f32[256,384]{0,1:T(8,128)S(1)} %get-tuple-element.62), channel_id=1, source_target_pairs={{0,1},{1,2},{2,3},{3,4},{4,5},{5,6},{6,7},{8,9},{9,10},{10,11},{11... | collective-permute-start | bytes 1179656 | tf_op jit(solution)/shard_map/ppermute | solution.py:14
  245.0 10.1 %collective-permute-start.15 = (f32[256,384]{0,1:T(8,128)S(1)}, f32[256,384]{0,1:T(8,128)S(1)}, u32[]{:S(2)}, u32[]{:S(2)}) collective-permute-start(f32[256,384]{0,1:T(8,128)S(1)} %get-tuple-element.31), channel_id=1, source_target_pairs={{1,0},{2,1},{3,2},{4,3},{5,4},{6,5},{7,6},{9,8},{10,9},{11,10},{12... | collective-permute-start | bytes 1179656 | tf_op jit(solution)/shard_map/ppermute | solution.py:14
  255.4 10.7 %collective-permute-start.14 = (f32[256,384]{0,1:T(8,128)S(1)}, f32[256,384]{0,1:T(8,128)S(1)}, u32[]{:S(2)}, u32[]{:S(2)}) collective-permute-start(f32[256,384]{0,1:T(8,128)S(1)} %get-tuple-element.60), channel_id=1, source_target_pairs={{0,1},{1,2},{2,3},{3,4},{4,5},{5,6},{6,7},{8,9},{9,10},{10,11},{11... | collective-permute-start | bytes 1179656 | tf_op jit(solution)/shard_map/ppermute | solution.py:14
  293.1 1.4 collective-permute-start.16
  294.4 4.9 %collective-permute-start.17 = (f32[64,384]{1,0:T(8,128)S(1)}, f32[64,384]{1,0:T(8,128)S(1)}, u32[]{:S(2)}, u32[]{:S(2)}) collective-permute-start(f32[64,384]{1,0:T(8,128)S(1)} %add.190), channel_id=1, source_target_pairs={{0,16},{8,24},{16,0},{24,8},{1,17},{9,25},{17,1},{25,9},{2,18},{10... | collective-permute-start | bytes 294920 | tf_op jit(solution)/shard_map/ppermute | solution.py:109
  322.9 11.9 %collective-permute-start.19 = (f32[256,384]{0,1:T(8,128)S(1)}, f32[256,384]{0,1:T(8,128)S(1)}, u32[]{:S(2)}, u32[]{:S(2)}) collective-permute-start(f32[256,384]{0,1:T(8,128)S(1)} %get-tuple-element.27), channel_id=1, source_target_pairs={{1,0},{2,1},{3,2},{4,3},{5,4},{6,5},{7,6},{9,8},{10,9},{11,10},{12... | collective-permute-start | bytes 1179656 | tf_op jit(solution)/shard_map/ppermute | solution.py:14
  335.0 11.9 %collective-permute-start.18 = (f32[256,384]{0,1:T(8,128)S(1)}, f32[256,384]{0,1:T(8,128)S(1)}, u32[]{:S(2)}, u32[]{:S(2)}) collective-permute-start(f32[256,384]{0,1:T(8,128)S(1)} %get-tuple-element.58), channel_id=1, source_target_pairs={{0,1},{1,2},{2,3},{3,4},{4,5},{5,6},{6,7},{8,9},{9,10},{10,11},{11... | collective-permute-start | bytes 1179656 | tf_op jit(solution)/shard_map/ppermute | solution.py:14
  348.4 10.1 %collective-permute-start.21 = (f32[256,384]{0,1:T(8,128)S(1)}, f32[256,384]{0,1:T(8,128)S(1)}, u32[]{:S(2)}, u32[]{:S(2)}) collective-permute-start(f32[256,384]{0,1:T(8,128)S(1)} %get-tuple-element.21), channel_id=1, source_target_pairs={{1,0},{2,1},{3,2},{4,3},{5,4},{6,5},{7,6},{9,8},{10,9},{11,10},{12... | collective-permute-start | bytes 1179656 | tf_op jit(solution)/shard_map/ppermute | solution.py:14
  358.9 10.7 %collective-permute-start.20 = (f32[256,384]{0,1:T(8,128)S(1)}, f32[256,384]{0,1:T(8,128)S(1)}, u32[]{:S(2)}, u32[]{:S(2)}) collective-permute-start(f32[256,384]{0,1:T(8,128)S(1)} %get-tuple-element.56), channel_id=1, source_target_pairs={{0,1},{1,2},{2,3},{3,4},{4,5},{5,6},{6,7},{8,9},{9,10},{10,11},{11... | collective-permute-start | bytes 1179656 | tf_op jit(solution)/shard_map/ppermute | solution.py:14
  369.8 26.9 %copy-start.24 = (f32[256,384]{0,1:T(8,128)}, f32[256,384]{0,1:T(8,128)S(1)}, u32[]{:S(2)}) copy-start(f32[256,384]{0,1:T(8,128)S(1)} %get-tuple-element.19) | copy-start | bytes 1179652
  396.7 1.4 collective-permute-start.22
  398.1 4.9 %collective-permute-start.23 = (f32[64,384]{1,0:T(8,128)S(1)}, f32[64,384]{1,0:T(8,128)S(1)}, u32[]{:S(2)}, u32[]{:S(2)}) collective-permute-start(f32[64,384]{1,0:T(8,128)S(1)} %add.199), channel_id=1, source_target_pairs={{0,16},{8,24},{16,0},{24,8},{1,17},{9,25},{17,1},{25,9},{2,18},{10... | collective-permute-start | bytes 294920 | tf_op jit(solution)/shard_map/ppermute | solution.py:109
  426.4 11.9 %collective-permute-start.25 = (f32[256,384]{0,1:T(8,128)S(1)}, f32[256,384]{0,1:T(8,128)S(1)}, u32[]{:S(2)}, u32[]{:S(2)}) collective-permute-start(f32[256,384]{0,1:T(8,128)S(1)} %get-tuple-element.17), channel_id=1, source_target_pairs={{1,0},{2,1},{3,2},{4,3},{5,4},{6,5},{7,6},{9,8},{10,9},{11,10},{12... | collective-permute-start | bytes 1179656 | tf_op jit(solution)/shard_map/ppermute | solution.py:14
  438.5 11.9 %collective-permute-start.24 = (f32[256,384]{0,1:T(8,128)S(1)}, f32[256,384]{0,1:T(8,128)S(1)}, u32[]{:S(2)}, u32[]{:S(2)}) collective-permute-start(f32[256,384]{0,1:T(8,128)S(1)} %get-tuple-element.54), channel_id=1, source_target_pairs={{0,1},{1,2},{2,3},{3,4},{4,5},{5,6},{6,7},{8,9},{9,10},{10,11},{11... | collective-permute-start | bytes 1179656 | tf_op jit(solution)/shard_map/ppermute | solution.py:14
  452.2 10.1 %collective-permute-start.27 = (f32[256,384]{0,1:T(8,128)S(1)}, f32[256,384]{0,1:T(8,128)S(1)}, u32[]{:S(2)}, u32[]{:S(2)}) collective-permute-start(f32[256,384]{0,1:T(8,128)S(1)} %get-tuple-element.11), channel_id=1, source_target_pairs={{1,0},{2,1},{3,2},{4,3},{5,4},{6,5},{7,6},{9,8},{10,9},{11,10},{12... | collective-permute-start | bytes 1179656 | tf_op jit(solution)/shard_map/ppermute | solution.py:14
  463.3 10.9 %collective-permute-start.26 = (f32[256,384]{0,1:T(8,128)}, f32[256,384]{0,1:T(8,128)}, u32[]{:S(2)}, u32[]{:S(2)}) collective-permute-start(f32[256,384]{0,1:T(8,128)} %get-tuple-element.52), channel_id=1, source_target_pairs={{0,1},{1,2},{2,3},{3,4},{4,5},{5,6},{6,7},{8,9},{9,10},{10,11},{11... | collective-permute-start | bytes 1179656 | tf_op jit(solution)/shard_map/ppermute | solution.py:14
  (48 other events, 361.0 us)
